TPU v7x, 32 devices: a whole 2x2x4 slice. The times are simulated.
32 devices in a mesh: expert: 4 (over z), tensor: 8 (over y, x, core).
Axes of the slice: x: 2, y: 2, z: 4, core: 2. Of those that a mesh axis runs over, the one named last changes fastest.
Arguments:
- expert_inputs: bfloat16 [8, 64, 4096], P('expert'), may hold values from -6 to 6
- gates: float32 [8, 64], P('expert'), may hold values from 0.2 to 1
- chosen_tokens: int32 [8, 64], replicated, may hold values from 0 to 4095, as said below
- w_gate: bfloat16 [8, 4096, 1792], P('expert', None, 'tensor'), may hold values from -0.09375 to 0.09375
- w_up: bfloat16 [8, 4096, 1792], P('expert', None, 'tensor'), may hold values from -0.09375 to 0.09375
- w_down: bfloat16 [8, 1792, 4096], P('expert', 'tensor'), may hold values from -0.125 to 0.125
- residual: bfloat16 [4096, 4096], P(('expert', 'tensor')), may hold values from -6 to 6
- norm_gain: float32 [4096], replicated, may hold values from 0.5 to 1.5
- w_qkv: bfloat16 [4096, 12288], P(None, 'tensor'), may hold values from -0.09375 to 0.09375
Outputs:
- stream: bfloat16 [4096, 4096], P(('expert', 'tensor'))
- projected: bfloat16 [4096, 12288], P('expert', 'tensor')
Inputs may be any that keep to these rules, and one draw needn't show every extreme that they name: `chosen_tokens`: each row holds 64 different token indices; at most 4 of a row lie in one block of 128 consecutive tokens, and in every draw some block holds 4 tokens of every row.
All inputs are finite; a program needn't handle non-finite values.
Results may differ from a plain program's by a relative error of at most 0.005.
Values may be sent and summed in bfloat16 or wider, within the bound.
No kernel may reach another device: no remote copies, remote signals or barrier semaphores. Data moves between devices by JAX's collectives and lax.ppermute only.
A program may use at most 128 MiB of HBM per device.

v0:
```python
import jax
import jax.numpy as jnp
from jax import lax
from jax.sharding import PartitionSpec as P

MOST = 4


def rank_within(target_owner):
    count_rows = target_owner.shape[0]
    same_owner = target_owner[:, None] == target_owner[None, :]
    earlier_rows = jnp.arange(count_rows)[None, :] < jnp.arange(count_rows)[:, None]
    return jnp.sum((same_owner & earlier_rows).astype(jnp.int32), axis=1)


def per_device(
    expert_inputs, gates, chosen_tokens, w_gate, w_up, w_down, residual, norm_gain, w_qkv
):
    expert_count = lax.axis_size("expert")
    tensor_count = lax.axis_size("tensor")
    devices_all = expert_count * tensor_count
    owner_index = lax.axis_index("expert") * tensor_count + lax.axis_index("tensor")
    local_experts = expert_inputs.shape[0]
    slot_count = expert_inputs.shape[1]
    feature_width = expert_inputs.shape[2]
    tok_rows = residual.shape[0]
    slot_depth = local_experts * MOST
    gate_part = jnp.einsum(
        "ecd,edf->ecf", expert_inputs, w_gate, preferred_element_type=jnp.float32
    )
    up_part = jnp.einsum("ecd,edf->ecf", expert_inputs, w_up, preferred_element_type=jnp.float32)
    hidden = (jax.nn.silu(gate_part) * up_part).astype(jnp.bfloat16)
    partial_value = (
        jnp.einsum("ecf,efd->ecd", hidden, w_down, preferred_element_type=jnp.float32)
        * gates[:, :, None]
    )
    expert_rows = partial_value.reshape(-1, feature_width)
    row_total = expert_rows.shape[0]
    my_tokens = lax.dynamic_slice_in_dim(
        chosen_tokens, lax.axis_index("expert") * local_experts, local_experts, 0
    ).reshape(-1)
    target_owner = my_tokens // tok_rows
    place_rank = rank_within(target_owner)
    sorting_key = target_owner % tensor_count * expert_count + target_owner // tensor_count
    target_slot = sorting_key * slot_depth + place_rank
    source = (
        jnp.full((devices_all * slot_depth,), row_total, jnp.int32)
        .at[target_slot]
        .set(jnp.arange(row_total, dtype=jnp.int32))
    )
    padded = jnp.concatenate([expert_rows, jnp.zeros((1, feature_width), jnp.float32)], axis=0)
    buffer = jnp.take(padded, source, axis=0)
    reduced = lax.psum_scatter(buffer, "tensor", scatter_dimension=0, tiled=True)
    arrived = lax.all_to_all(
        reduced.reshape(expert_count, slot_depth, feature_width),
        "expert",
        split_axis=0,
        concat_axis=0,
        tiled=True,
    )
    accumulated_rows = arrived.reshape(expert_count * slot_depth, feature_width)
    group_tokens = chosen_tokens.reshape(expert_count, local_experts * slot_count)
    group_owner = group_tokens // tok_rows
    group_rank = jax.vmap(rank_within)(group_owner)
    is_mine = group_owner == owner_index
    group_key = jnp.where(
        is_mine,
        jnp.arange(expert_count, dtype=jnp.int32)[:, None] * slot_depth + group_rank,
        expert_count * slot_depth,
    )
    slot_offset = (
        jnp.full((expert_count * slot_depth,), -1, jnp.int32)
        .at[group_key.reshape(-1)]
        .set((group_tokens % tok_rows).reshape(-1), mode="drop")
    )
    placement_table = (
        jnp.arange(tok_rows, dtype=jnp.int32)[:, None] == slot_offset[None, :]
    ).astype(jnp.float32)
    combined = residual.astype(jnp.float32) + jnp.dot(
        placement_table,
        accumulated_rows,
        precision=lax.Precision.HIGHEST,
        preferred_element_type=jnp.float32,
    )
    stream = combined.astype(jnp.bfloat16)
    scale_rows = lax.rsqrt(jnp.mean(combined * combined, axis=-1, keepdims=True) + 1e-06)
    normed = (combined * scale_rows * norm_gain[None, :]).astype(jnp.bfloat16)
    projected = jnp.dot(
        lax.all_gather(normed, "tensor", axis=0, tiled=True),
        w_qkv,
        preferred_element_type=jnp.float32,
    ).astype(jnp.bfloat16)
    return (stream, projected)


def solution(mesh):
    return jax.shard_map(
        per_device,
        mesh=mesh,
        in_specs=(
            P("expert", None, None),
            P("expert", None),
            P(),
            P("expert", None, "tensor"),
            P("expert", None, "tensor"),
            P("expert", "tensor", None),
            P(("expert", "tensor"), None),
            P(),
            P(None, "tensor"),
        ),
        out_specs=(P(("expert", "tensor"), None), P("expert", "tensor")),
        check_vma=False,
    )
```

profile of v0, /device:TPU:0, one launch (start us, length us, event | category | flops | bytes accessed | tf_op | source)
XLA Modules:
  0.0 184.1 jit_solution(11455417475515096686)
XLA Ops:
  7.2 0.8 constant_dynamic-slice_fusion
  8.0 0.1 reshape.423
  8.1 0.1 reshape.422
  8.2 0.2 convert_reduce_fusion.1
  8.4 1.0 scatter_custom_fusion.1
  9.4 3.3 %fusion.20 = f32[2,64,224]{2,1,0:T(8,128)S(1)} fusion(bf16[2,64,4096]{2,1,0:T(8,128)(2,1)S(1)} %copy-done, bf16[2,4096,224]{1,2,0:T(8,128)(2,1)} %param.12), kind=kOutput, calls=%fused_computation.70 | convolution fusion | flops 234881024 | bytes 4833280 | tf_op jit(solution)/shard_map/ecd,edf->ecf/dot_general | solution.py:28
  12.7 6.5 %convolution_multiply_fusion = f32[2,64,4096]{2,1,0:T(8,128)} fusion(bf16[2,224,4096]{2,1,0:T(8,128)(2,1)} %param.14, bf16[2,64,4096]{2,1,0:T(8,128)(2,1)S(1)} %copy-done, bf16[2,4096,224]{1,2,0:T(8,128)(2,1)} %param.13, f32[2,64]{1,0:T(2,128)S(1)} %copy-done.4, f32[2,64,224]{2,1,0:T(8,128)S(1)} %fusion.20), kind=kOutput, calls=%fused_computation.4 | convolution fusion | flops 470458368 | bytes 10600960 | tf_op jit(solution)/shard_map/ecf,efd->ecd/dot_general | solution.py:34
  19.2 1.8 concatenate.3
  21.1 3.8 %gather_fusion = f32[256,4096]{1,0:T(8,128)} fusion(f32[129,4096]{1,0:T(8,128)S(1)} %concatenate.3, s32[1024]{0:T(1024)S(1)} %pad_clamp_fusion), kind=kCustom, calls=%fused_computation | custom fusion | bytes 8389632 | tf_op jit(solution)/shard_map/jit(_take)/gather | solution.py:52
  24.9 4.7 %broadcast_select_fusion = f32[256,4096]{1,0:T(8,128)} fusion(f32[256,4096]{1,0:T(8,128)} %gather_fusion, pred[256]{0:T(512)(128)(4,1)S(1)} %compare_and_fusion), kind=kLoop, calls=%fused_computation.8 | loop fusion | flops 1048576 | bytes 8388864 | tf_op jit(solution)/shard_map/jit(_take)/select_n | solution.py:52
  29.6 0.7 copy-done.2
  30.3 0.1 reshape.420
  30.4 53.3 %reduce-scatter.2.cloned.1.call-done = f32[32,4096]{1,0:T(8,128)} async-done(((f32[256,4096]{1,0:T(8,128)}), f32[32,4096]{1,0:T(8,128)}) %reduce-scatter.2.cloned.1.call-update) | async-done | bytes 524304 | tf_op jit(solution)/shard_map/reduce_scatter | solution.py:53
  83.7 4.6 %all-to-all-start = ((f32[4,8,4096]{2,1,0:T(8,128)}), f32[4,8,4096]{2,1,0:T(8,128)S(1)}, u32[]{:S(2)}, u32[]{:S(2)}) async-start(f32[4,8,4096]{2,1,0:T(8,128)} %bitcast.25), calls=%async_computation.1 | async-start | bytes 1048576 | tf_op jit(solution)/shard_map/all_to_all | solution.py:54
  88.2 0.2 convert_reduce_fusion
  88.5 0.1 reshape.419
  88.6 0.1 reshape.421
  88.7 0.1 broadcast_add_fusion
  88.8 2.4 %scatter_custom_fusion = s32[32]{0:T(128)S(1)} fusion(s32[512]{0:T(512)S(1)} %bitcast.27, s32[512]{0:T(512)S(1)} %add_select_fusion, s32[]{:T(128)} %constant.88.clone.1), kind=kCustom, calls=%fused_computation.67 | custom fusion | bytes 132 | tf_op jit(solution)/shard_map/scatter | solution.py:74
  91.2 11.4 %all-to-all-done = f32[4,8,4096]{2,1,0:T(8,128)S(1)} async-done(((f32[4,8,4096]{2,1,0:T(8,128)}), f32[4,8,4096]{2,1,0:T(8,128)S(1)}, u32[]{:S(2)}, u32[]{:S(2)}) %all-to-all-start) | async-done | bytes 524320 | tf_op jit(solution)/shard_map/all_to_all | solution.py:54
  102.6 1.3 multiply_reduce_fusion
  103.9 1.7 multiply_convert_fusion
  105.6 52.5 %all-gather.2.cloned.1.call-done = bf16[1024,4096]{1,0:T(8,128)(2,1)} async-done(((bf16[128,4096]{1,0:T(8,128)(2,1)}), bf16[1024,4096]{1,0:T(8,128)(2,1)}) %all-gather.2.cloned.1.call-update) | async-done | bytes 8388624 | tf_op jit(solution)/shard_map/all_gather | solution.py:89
  158.1 19.1 %convolution_convert_fusion = bf16[1024,1536]{1,0:T(8,128)(2,1)} fusion(bf16[1024,4096]{1,0:T(8,128)(2,1)} %all-gather.2.cloned.1.call-done, bf16[4096,1536]{1,0:T(8,128)(2,1)} %param.17), kind=kOutput, calls=%fused_computation.5 | convolution fusion | flops 12886474752 | bytes 24117248 | tf_op jit(solution)/shard_map/dot_general | solution.py:88
  (25 shorter events, 0.2 us)
Async XLA Ops:
  7.2 2.3 %copy-start = (bf16[2,64,4096]{2,1,0:T(8,128)(2,1)S(1)}, bf16[2,64,4096]{2,1,0:T(8,128)(2,1)}, u32[]{:S(2)}) copy-start(bf16[2,64,4096]{2,1,0:T(8,128)(2,1)} %param.9) | copy-start | bytes 3145732
  7.2 5.6 %copy-start.4 = (f32[2,64]{1,0:T(2,128)S(1)}, f32[2,64]{1,0:T(2,128)}, u32[]{:S(2)}) copy-start(f32[2,64]{1,0:T(2,128)} %param.10) | copy-start | bytes 1540
  7.2 76.5 %reduce-scatter.2.cloned.1.call-start = ((), (), s32[]{:S(2)}) async-start(), calls=%async_computation.2 | async-start | bytes 4718592 | tf_op jit(solution)/shard_map/reduce_scatter | solution.py:53
  29.6 0.7 copy-start.2
  29.6 73.0 %copy-start.1 = (bf16[128,4096]{1,0:T(8,128)(2,1)S(1)}, bf16[128,4096]{1,0:T(8,128)(2,1)}, u32[]{:S(2)}) copy-start(bf16[128,4096]{1,0:T(8,128)(2,1)} %param.15) | copy-start | bytes 3145732
  29.6 74.3 %copy-start.3 = (f32[4096]{0:T(1024)S(1)}, f32[4096]{0:T(1024)}, u32[]{:S(2)}) copy-start(f32[4096]{0:T(1024)} %param.16) | copy-start | bytes 49156
  83.7 18.9 %all-to-all-start = ((f32[4,8,4096]{2,1,0:T(8,128)}), f32[4,8,4096]{2,1,0:T(8,128)S(1)}, u32[]{:S(2)}, u32[]{:S(2)}) async-start(f32[4,8,4096]{2,1,0:T(8,128)} %bitcast.25), calls=%async_computation.1 | async-start | bytes 1048576 | tf_op jit(solution)/shard_map/all_to_all | solution.py:54
  88.2 69.8 %all-gather.2.cloned.1.call-start = ((), (), s32[]{:S(2)}) async-start(), calls=%async_computation.3 | async-start | bytes 9437184 | tf_op jit(solution)/shard_map/all_gather | solution.py:89
Sparse Core Ops, SparseCore 0:
  29.7 53.8 reduce-scatter.1
  105.7 52.3 all-gather.1
where the time goes:
time: 184 us
  waiting for transfers between devices  117 us (64%)
  matrix products  30.2 us (16%)
  between operations  14.2 us (8%)
  local copies, waits for them, and re-layouts  10.9 us (6%)
  other arithmetic  6.99 us (4%)
  starting transfers between devices  4.62 us (3%)
    reduce_scatter x1, waiting for transfers between devices, per_device(): lax.psum_scatter(buffer, 'tensor', scatter_dimension=0, tiled=True)  53.3 us
    all_gather x1, waiting for transfers between devices, per_device(): lax.all_gather(normed, 'tensor', axis=0, tiled=True)  52.5 us
    dot_general x1, matrix products, per_device(): jnp.dot(lax.all_gather(normed, 'tensor', axis=0, tiled=True), w_qkv, pref...  19.1 us
    all_to_all x1, waiting for transfers between devices, per_device(): lax.all_to_all(reduced.reshape(expert_count, slot_depth, feature_width),...  11.4 us
    dot_general x1, matrix products, per_device(): jnp.einsum('ecf,efd->ecd', hidden, w_down, preferred_element_type=jnp.flo...  6.48 us
    select_n x2, other arithmetic, per_device(): buffer = jnp.take(padded, source, axis=0)  4.7 us
    all_to_all x1, starting transfers between devices, per_device(): lax.all_to_all(reduced.reshape(expert_count, slot_depth, feature_width),...  4.58 us
    gather x1, local copies, waits for them, and re-layouts, per_device(): buffer = jnp.take(padded, source, axis=0)  3.83 us
  transfers between devices with their start and end apart: 3, of which 3 were waited for; matrix products, arithmetic and copies ran while one was open for 2% of the time, Pallas kernels for 0%

commit v1 on v0

v1 whole, which is shorter than its diff:
```python
import jax
import jax.numpy as jnp
from jax import lax
from jax.experimental import pallas as pl
from jax.experimental.pallas import tpu as pltpu
from jax.sharding import PartitionSpec as P


MOST = 4
CHUNKS = 4


def column_tile(columns):
    for tile in (512, 384, 256, 128):
        if columns % tile == 0:
            return tile
    return columns


def stream_kernel(rows, base, slots, contributions, out):
    row_total = rows.shape[0]
    token = base[0] + lax.broadcasted_iota(jnp.int32, (row_total, slots.shape[1]), 0)
    table = (token == slots[...]).astype(jnp.bfloat16)
    added = jnp.dot(table, contributions[0], preferred_element_type=jnp.float32)
    out[...] = (rows[...].astype(jnp.float32) + added).astype(jnp.bfloat16)


def make_stream(residual, base, token_of_slot, contributions):
    blocks, slots, part = contributions.shape
    row_total, width = residual.shape
    return pl.pallas_call(
        stream_kernel,
        grid=(blocks,),
        in_specs=[
            pl.BlockSpec((row_total, part), lambda t: (0, t)),
            pl.BlockSpec(memory_space=pltpu.SMEM),
            pl.BlockSpec((1, slots), lambda t: (0, 0)),
            pl.BlockSpec((1, slots, part), lambda t: (t, 0, 0)),
        ],
        out_specs=pl.BlockSpec((row_total, part), lambda t: (0, t)),
        out_shape=jax.ShapeDtypeStruct((row_total, width), jnp.bfloat16),
        cost_estimate=pl.CostEstimate(
            flops=2 * row_total * slots * width, bytes_accessed=4 << 20, transcendentals=0
        ),
        name="stream_rows",
    )(residual, base, token_of_slot, contributions)


def project_chunk(chunk, tok_rows, rows, token_of_slot, contributions, gain, weights, target):
    blocks, slots, part = contributions.shape
    row_total, width = rows.shape
    chunk_rows = row_total // blocks
    columns = weights.shape[1]
    tile = column_tile(columns)

    def kernel(rows_ref, slots_ref, contributions_ref, gain_ref, weights_ref, *rest):
        out, combined, normed = rest[-3:]

        @pl.when(pl.program_id(0) == 0)
        def _():
            row = lax.broadcasted_iota(jnp.int32, (row_total, slots), 0)
            token = (row // chunk_rows) * tok_rows + chunk * chunk_rows + row % chunk_rows
            table = (token == slots_ref[...]).astype(jnp.bfloat16)
            squares = jnp.zeros((row_total, 1), jnp.float32)
            for t in range(blocks):
                at = slice(t * part, (t + 1) * part)
                value = rows_ref[:, at].astype(jnp.float32) + jnp.dot(
                    table, contributions_ref[t], preferred_element_type=jnp.float32
                )
                combined[:, at] = value
                squares = squares + jnp.sum(value * value, axis=1, keepdims=True)
            scale = lax.rsqrt(squares / width + 1e-06)
            for t in range(blocks):
                at = slice(t * part, (t + 1) * part)
                normed[:, at] = (combined[:, at] * scale * gain_ref[:, at]).astype(jnp.bfloat16)

        value = jnp.dot(normed[...], weights_ref[...], preferred_element_type=jnp.float32)
        out[...] = value.astype(jnp.bfloat16).reshape(blocks, chunk_rows, tile)

    in_specs = [
        pl.BlockSpec((row_total, width), lambda n: (0, 0)),
        pl.BlockSpec((1, slots), lambda n: (0, 0)),
        pl.BlockSpec((blocks, slots, part), lambda n: (0, 0, 0)),
        pl.BlockSpec((1, width), lambda n: (0, 0)),
        pl.BlockSpec((width, tile), lambda n: (0, n)),
    ]
    operands = [rows, token_of_slot, contributions, gain, weights]
    aliases = {}
    if target is not None:
        in_specs.append(pl.BlockSpec(memory_space=pl.ANY))
        operands.append(target)
        aliases = {5: 0}
    return pl.pallas_call(
        kernel,
        grid=(columns // tile,),
        in_specs=in_specs,
        out_specs=pl.BlockSpec((blocks, chunk_rows, tile), lambda n: (0, chunk, n)),
        out_shape=jax.ShapeDtypeStruct((blocks, tok_rows, columns), jnp.bfloat16),
        scratch_shapes=[
            pltpu.VMEM((row_total, width), jnp.float32),
            pltpu.VMEM((row_total, width), jnp.bfloat16),
        ],
        input_output_aliases=aliases,
        cost_estimate=pl.CostEstimate(
            flops=2 * row_total * width * (columns + slots),
            bytes_accessed=2 * width * columns,
            transcendentals=0,
        ),
        compiler_params=pltpu.CompilerParams(vmem_limit_bytes=58 << 20),
        name="project_rows",
    )(*operands)


def layer(
    expert_inputs, gates, chosen_tokens, w_gate, w_up, w_down, residual, norm_gain, w_qkv
):
    expert_count = lax.axis_size("expert")
    tensor_count = lax.axis_size("tensor")
    group_index = lax.axis_index("expert")
    tensor_index = lax.axis_index("tensor")
    local_experts, slot_count, feature_width = expert_inputs.shape
    tok_rows = residual.shape[0]
    group_rows = tok_rows * tensor_count
    total_experts = expert_count * local_experts
    local_rows = local_experts * slot_count
    feature_part = feature_width // tensor_count
    chunk_rows = tok_rows // CHUNKS

    gathered = []
    for c in range(CHUNKS):
        piece = residual[c * chunk_rows : (c + 1) * chunk_rows]
        gathered.append(lax.all_gather(piece, "tensor", axis=0, tiled=True))

    in_group = (chosen_tokens // group_rows) == group_index
    rank = jnp.cumsum(in_group.astype(jnp.int32), axis=1) - 1
    per_expert = min(MOST * tensor_count, slot_count)
    compact_rows = total_experts * per_expert
    slot = jnp.where(
        in_group,
        jnp.arange(total_experts, dtype=jnp.int32)[:, None] * per_expert + rank,
        compact_rows,
    ).reshape(-1)
    pick = jnp.arange(compact_rows, dtype=jnp.int32)[:, None] == slot[None, :]
    local_token = (chosen_tokens % group_rows).reshape(-1)
    token_of_slot = jnp.sum(jnp.where(pick, local_token[None, :] + 1, 0), axis=1) - 1
    pick = pick.astype(jnp.bfloat16)

    gate_part = jnp.einsum(
        "ecd,edf->ecf", expert_inputs, w_gate, preferred_element_type=jnp.float32
    )
    up_part = jnp.einsum("ecd,edf->ecf", expert_inputs, w_up, preferred_element_type=jnp.float32)
    hidden = (jax.nn.silu(gate_part) * up_part).astype(jnp.bfloat16)
    partial_value = (
        jnp.einsum("ecf,efd->ecd", hidden, w_down, preferred_element_type=jnp.float32)
        * gates[:, :, None]
    ).astype(jnp.bfloat16)
    partial_rows = partial_value.reshape(local_rows, feature_width)

    blocks = lax.all_to_all(
        partial_rows, "tensor", split_axis=1, concat_axis=0, tiled=True
    ).reshape(tensor_count, local_rows, feature_part)
    summed = lax.optimization_barrier(jnp.sum(blocks.astype(jnp.float32), axis=0))
    every_row = lax.all_gather(summed.astype(jnp.bfloat16), "expert", axis=0, tiled=True)
    compact = jnp.dot(pick, every_row, preferred_element_type=jnp.float32).astype(jnp.bfloat16)
    contributions = lax.all_gather(compact, "tensor", axis=0, tiled=False)

    base = (tensor_index * tok_rows).astype(jnp.int32).reshape(1)
    slots = token_of_slot.reshape(1, compact_rows)
    gain = norm_gain.reshape(1, feature_width)
    stream = make_stream(residual, base, slots, contributions)
    projected = None
    for c in range(CHUNKS):
        projected = project_chunk(
            c, tok_rows, gathered[c], slots, contributions, gain, w_qkv, projected
        )
    return (stream, projected.reshape(group_rows, -1))


def solution(mesh):
    return jax.shard_map(
        layer,
        mesh=mesh,
        in_specs=(
            P("expert", None, None),
            P("expert", None),
            P(),
            P("expert", None, "tensor"),
            P("expert", None, "tensor"),
            P("expert", "tensor", None),
            P(("expert", "tensor"), None),
            P(),
            P(None, "tensor"),
        ),
        out_specs=(P(("expert", "tensor"), None), P("expert", "tensor")),
        check_vma=False,
    )
```

time: 184 us -> 221 us (1.20)
  Pallas kernels: 0 us -> 47.3 us
  matrix products: 30.2 us -> 9.47 us
  blocking collectives: 0 us -> 16.1 us
  local copies, waits for them, and re-layouts: 10.9 us -> 4.05 us
  other arithmetic: 6.99 us -> 1.12 us
  waiting for transfers between devices: 117 us -> 122 us
    all_gather x1 -> x5, waiting for transfers between devices: 52.5 us -> 106 us  [the longest x4 82.1 us: layer(): gathered.append(lax.all_gather(piece, 'tensor', axis=0, tiled=True))]
    reduce_scatter x1 -> x0, waiting for transfers between devices: 53.3 us -> none  [per_device(): lax.psum_scatter(buffer, 'tensor', scatter_dimension=0, tiled=True)]
    pallas_call x0 -> x5, Pallas kernels: none -> 47.3 us  [the longest x4 40.9 us: project_chunk(): pl.pallas_call(kernel, grid=(columns // tile,), in_specs=in_specs, out_sp...]
    dot_general x4 -> x3, matrix products: 30.2 us -> 9.47 us  [the longest x1 5.16 us: layer(): jnp.einsum('ecf,efd->ecd', hidden, w_down, preferred_element_type=jnp.flo...]
    all_gather x0 -> x1, blocking collectives: none -> 16.1 us  [layer(): lax.all_gather(summed.astype(jnp.bfloat16), 'expert', axis=0, tiled=True)]
    select_n x7 -> x1, other arithmetic: 4.78 us -> 0.07 us  [layer(): jnp.where(in_group, jnp.arange(total_experts, dtype=jnp.int32)[:, None] *...]
    gather x1 -> x0, local copies, waits for them, and re-layouts: 3.83 us -> none  [per_device(): buffer = jnp.take(padded, source, axis=0)]
    all_to_all x1, waiting for transfers between devices: 11.4 us -> 14.9 us  [layer(): lax.all_to_all(partial_rows, 'tensor', split_axis=1, concat_axis=0, tiled...]
  transfers between devices with their start and end apart: 3 -> 6, of which waited for: 3 -> 6; matrix products, arithmetic and copies ran while one was open for 2% -> 1% of each run, Pallas kernels for 0% -> 17%
where the time goes in v1:
time: 221 us; the launch traced here: 220 us
  waiting for transfers between devices  122 us (55%)
  Pallas kernels  47.3 us (21%)
  blocking collectives  16.1 us (7%)
  between operations  13.9 us (6%)
  matrix products  9.47 us (4%)
  starting transfers between devices  5.57 us (3%)
  local copies, waits for them, and re-layouts  4.05 us (2%)
    all_gather x4, waiting for transfers between devices, layer(): gathered.append(lax.all_gather(piece, 'tensor', axis=0, tiled=True))  82.1 us
    pallas_call x4, Pallas kernels, project_chunk(): pl.pallas_call(kernel, grid=(columns // tile,), in_specs=in_specs, out_sp...  40.9 us
    all_gather x1, waiting for transfers between devices, layer(): contributions = lax.all_gather(compact, 'tensor', axis=0, tiled=False)  23.9 us
    all_gather x1, blocking collectives, layer(): lax.all_gather(summed.astype(jnp.bfloat16), 'expert', axis=0, tiled=True)  16.1 us
    all_to_all x1, waiting for transfers between devices, layer(): lax.all_to_all(partial_rows, 'tensor', split_axis=1, concat_axis=0, tiled...  14.9 us
    pallas_call x1, Pallas kernels, make_stream(): pl.pallas_call(stream_kernel, grid=(blocks,), in_specs=[pl.BlockSpec((row...  6.37 us
    all_to_all x1, starting transfers between devices, layer(): lax.all_to_all(partial_rows, 'tensor', split_axis=1, concat_axis=0, tiled...  5.19 us
    dot_general x1, matrix products, layer(): jnp.einsum('ecf,efd->ecd', hidden, w_down, preferred_element_type=jnp.flo...  5.16 us
  transfers between devices with their start and end apart: 6, of which 6 were waited for; matrix products, arithmetic and copies ran while one was open for 1% of the time, Pallas kernels for 17%

profile of v1, /device:TPU:0, one launch (start us, length us, event | category | flops | bytes accessed | tf_op | source)
XLA Modules:
  0.0 219.9 jit_solution(13757401975003861995)
XLA Ops:
  7.2 1.2 copy-done
  8.4 3.3 %fusion.17 = f32[2,64,224]{2,1,0:T(8,128)S(1)} fusion(bf16[2,64,4096]{2,1,0:T(8,128)(2,1)S(1)} %copy-done, bf16[2,4096,224]{1,2,0:T(8,128)(2,1)} %param.12), kind=kOutput, calls=%fused_computation.31 | convolution fusion | flops 234881024 | bytes 4833280 | tf_op jit(solution)/shard_map/ecd,edf->ecf/dot_general | solution.py:148
  11.7 5.2 %fusion = bf16[2,64,4096]{2,1,0:T(8,128)(2,1)S(1)} fusion(bf16[2,224,4096]{2,1,0:T(8,128)(2,1)} %param.14, bf16[2,64,4096]{2,1,0:T(8,128)(2,1)S(1)} %copy-done, bf16[2,4096,224]{1,2,0:T(8,128)(2,1)} %param.13, f32[2,64]{1,0:T(2,128)S(1)} %copy-done.3, f32[2,64,224]{2,1,0:T(8,128)S(1)} %fusion.17), kind=kOutput, calls=%fused_computation.1 | convolution fusion | flops 470982656 | bytes 9552384 | tf_op jit(solution)/shard_map/ecf,efd->ecd/dot_general | solution.py:154
  16.9 0.4 copy.16
  17.3 1.3 copy.15
  18.6 5.2 %all-to-all-start = ((bf16[128,8,512]{2,0,1:T(8,128)(2,1)}), bf16[128,8,512]{2,0,1:T(8,128)(2,1)S(1)}, u32[]{:S(2)}, u32[]{:S(2)}) async-start(bf16[128,8,512]{2,0,1:T(8,128)(2,1)} %copy.15), calls=%async_computation | async-start | bytes 2097152 | tf_op jit(solution)/shard_map/all_to_all | solution.py:159
  24.2 14.9 %all-to-all-done = bf16[128,8,512]{2,0,1:T(8,128)(2,1)S(1)} async-done(((bf16[128,8,512]{2,0,1:T(8,128)(2,1)}), bf16[128,8,512]{2,0,1:T(8,128)(2,1)S(1)}, u32[]{:S(2)}, u32[]{:S(2)}) %all-to-all-start) | async-done | bytes 1048608 | tf_op jit(solution)/shard_map/all_to_all | solution.py:159
  39.3 16.1 %all_gather.21 = bf16[512,512]{1,0:T(8,128)(2,1)S(1)} all-gather(bf16[128,512]{1,0:T(8,128)(2,1)S(1)} %convert_reduce_fusion), channel_id=1, replica_groups=mesh['expert'=4,'tensor'=8] {'expert'}, dimensions={0}, use_global_device_ids=true | all-gather | bytes 655360 | tf_op jit(solution)/shard_map/all_gather | solution.py:163
  55.4 1.0 convolution_convert_fusion
  56.5 1.0 fusion.16
  57.6 0.7 all-gather.11.cloned.1.call-update
  58.3 0.5 all-gather.9.cloned.1.call-update
  59.1 0.4 all-gather.7.cloned.1.call-update
  59.7 0.5 broadcast_add_fusion
  60.2 23.9 %all-gather.15.cloned.1.call-done = bf16[2048,512]{1,0:T(8,128)(2,1)} async-done(((bf16[256,512]{1,0:T(8,128)(2,1)}), bf16[2048,512]{1,0:T(8,128)(2,1)}) %all-gather.15.cloned.1.call-update) | async-done | bytes 2097168 | tf_op jit(solution)/shard_map/all_gather | solution.py:165
  84.1 6.4 %stream_rows.1 = bf16[128,4096]{1,0:T(8,128)(2,1)} custom-call(bf16[128,4096]{1,0:T(8,128)(2,1)} %rows.1, s32[1]{0:T(128)} %bitcast.base, s32[1,256]{1,0:T(1,128)} %bitcast.26, bf16[8,256,512]{2,1,0:T(8,128)(2,1)} %bitcast.14), custom_call_target="tpu_custom_call" | custom-call | flops 268435456 | bytes 4194304 | tf_op jit(solution)/shard_map/stream_rows/pallas_call | solution.py:31
  90.4 23.9 %all-gather.13.cloned.1.call-done.rows_ref = bf16[256,4096]{1,0:T(8,128)(2,1)} async-done(((bf16[32,4096]{1,0:T(8,128)(2,1)}), bf16[256,4096]{1,0:T(8,128)(2,1)}) %all-gather.13.cloned.1.call-update) | async-done | bytes 2097168 | tf_op jit(solution)/shard_map/all_gather | solution.py:132
  114.3 10.2 %project_rows.4.rest_0_ = bf16[8,128,1536]{2,1,0:T(8,128)(2,1)} custom-call(bf16[256,4096]{1,0:T(8,128)(2,1)} %all-gather.13.cloned.1.call-done.rows_ref, s32[1,256]{1,0:T(1,128)} %bitcast.27, bf16[8,256,512]{2,1,0:T(8,128)(2,1)} %bitcast.15, f32[1,4096]{1,0:T(1,128)} %bitcast.22, bf16[4096,1536]{1,0:T(8,128)(2,1)} %weights_ref.7), custom_call_target="tpu_custom_call" | custom-call | flops 3758096384 | bytes 12582912 | tf_op jit(solution)/shard_map/project_rows/pallas_call | solution.py:93
  124.6 19.5 %all-gather.11.cloned.1.call-done.rows_ref = bf16[256,4096]{1,0:T(8,128)(2,1)} async-done(((bf16[32,4096]{1,0:T(8,128)(2,1)}), bf16[256,4096]{1,0:T(8,128)(2,1)}) %all-gather.11.cloned.1.call-update) | async-done | bytes 2097168 | tf_op jit(solution)/shard_map/all_gather | solution.py:132
  144.0 10.2 %project_rows.5.rest_0_ = bf16[8,128,1536]{2,1,0:T(8,128)(2,1)} custom-call(bf16[256,4096]{1,0:T(8,128)(2,1)} %all-gather.11.cloned.1.call-done.rows_ref, s32[1,256]{1,0:T(1,128)} %bitcast.28, bf16[8,256,512]{2,1,0:T(8,128)(2,1)} %bitcast.16, f32[1,4096]{1,0:T(1,128)} %bitcast.23, bf16[4096,1536]{1,0:T(8,128)(2,1)} %weights_ref.7, ...), custom_call_target="tpu_custom_call", output_to_operand_aliasing={{}: (5, {})} | custom-call | flops 3758096384 | bytes 12582912 | tf_op jit(solution)/shard_map/project_rows/pallas_call | solution.py:93
  154.3 19.3 %all-gather.9.cloned.1.call-done.rows_ref = bf16[256,4096]{1,0:T(8,128)(2,1)} async-done(((bf16[32,4096]{1,0:T(8,128)(2,1)}), bf16[256,4096]{1,0:T(8,128)(2,1)}) %all-gather.9.cloned.1.call-update) | async-done | bytes 2097168 | tf_op jit(solution)/shard_map/all_gather | solution.py:132
  173.6 10.2 %project_rows.6.rest_0_ = bf16[8,128,1536]{2,1,0:T(8,128)(2,1)} custom-call(bf16[256,4096]{1,0:T(8,128)(2,1)} %all-gather.9.cloned.1.call-done.rows_ref, s32[1,256]{1,0:T(1,128)} %bitcast.29, bf16[8,256,512]{2,1,0:T(8,128)(2,1)} %bitcast.17, f32[1,4096]{1,0:T(1,128)} %bitcast.24, bf16[4096,1536]{1,0:T(8,128)(2,1)} %weights_ref.7, ...), custom_call_target="tpu_custom_call", output_to_operand_aliasing={{}: (5, {})} | custom-call | flops 3758096384 | bytes 12582912 | tf_op jit(solution)/shard_map/project_rows/pallas_call | solution.py:93
  183.8 19.3 %all-gather.7.cloned.1.call-done.rows_ref = bf16[256,4096]{1,0:T(8,128)(2,1)} async-done(((bf16[32,4096]{1,0:T(8,128)(2,1)}), bf16[256,4096]{1,0:T(8,128)(2,1)}) %all-gather.7.cloned.1.call-update) | async-done | bytes 2097168 | tf_op jit(solution)/shard_map/all_gather | solution.py:132
  203.2 10.2 %project_rows.7 = bf16[8,128,1536]{2,1,0:T(8,128)(2,1)} custom-call(bf16[256,4096]{1,0:T(8,128)(2,1)} %all-gather.7.cloned.1.call-done.rows_ref, s32[1,256]{1,0:T(1,128)} %bitcast.30, bf16[8,256,512]{2,1,0:T(8,128)(2,1)} %bitcast.18, f32[1,4096]{1,0:T(1,128)} %bitcast.25, bf16[4096,1536]{1,0:T(8,128)(2,1)} %weights_ref.7, ...), custom_call_target="tpu_custom_call", output_to_operand_aliasing={{}: (5, {})} | custom-call | flops 3758096384 | bytes 12582912 | tf_op jit(solution)/shard_map/project_rows/pallas_call | solution.py:93
  (23 shorter events, 1.2 us)
Async XLA Ops:
  7.2 1.2 copy-start
  7.2 4.5 %copy-start.3 = (f32[2,64]{1,0:T(2,128)S(1)}, f32[2,64]{1,0:T(2,128)}, u32[]{:S(2)}) copy-start(f32[2,64]{1,0:T(2,128)} %param.10) | copy-start | bytes 1540
  16.9 7.0 %copy-start.2 = (s32[8,64]{1,0:T(8,128)S(1)}, s32[8,64]{1,0:T(8,128)}, u32[]{:S(2)}) copy-start(s32[8,64]{1,0:T(8,128)} %param.11) | copy-start | bytes 6148
  17.3 39.2 %copy-start.1 = (bf16[128,4096]{1,0:T(8,128)(2,1)S(1)}, bf16[128,4096]{1,0:T(8,128)(2,1)}, u32[]{:S(2)}) copy-start(bf16[128,4096]{1,0:T(8,128)(2,1)} %rows.1) | copy-start | bytes 3145732
  18.6 20.6 %all-to-all-start = ((bf16[128,8,512]{2,0,1:T(8,128)(2,1)}), bf16[128,8,512]{2,0,1:T(8,128)(2,1)S(1)}, u32[]{:S(2)}, u32[]{:S(2)}) async-start(bf16[128,8,512]{2,0,1:T(8,128)(2,1)} %copy.15), calls=%async_computation | async-start | bytes 2097152 | tf_op jit(solution)/shard_map/all_to_all | solution.py:159
  23.8 60.3 %all-gather.15.cloned.1.call-start = ((), (), s32[]{:S(2)}) async-start(), calls=%async_computation.5 | async-start | bytes 2359296 | tf_op jit(solution)/shard_map/all_gather | solution.py:165
  56.5 57.9 %all-gather.13.cloned.1.call-start = ((), (), s32[]{:S(2)}) async-start(), calls=%async_computation.4 | async-start | bytes 2359296 | tf_op jit(solution)/shard_map/all_gather | solution.py:132
  57.5 86.5 %all-gather.11.cloned.1.call-start = ((), (), s32[]{:S(2)}) async-start(), calls=%async_computation.3 | async-start | bytes 2359296 | tf_op jit(solution)/shard_map/all_gather | solution.py:132
  58.3 115.3 %all-gather.9.cloned.1.call-start = ((), (), s32[]{:S(2)}) async-start(), calls=%async_computation.2 | async-start | bytes 2359296 | tf_op jit(solution)/shard_map/all_gather | solution.py:132
  58.9 144.3 %all-gather.7.cloned.1.call-start = ((), (), s32[]{:S(2)}) async-start(), calls=%async_computation.1 | async-start | bytes 2359296 | tf_op jit(solution)/shard_map/all_gather | solution.py:132
Sparse Core Ops, SparseCore 0:
  56.6 27.4 all-gather.14
  86.5 27.7 all-gather.12
  116.2 27.7 all-gather.10
  145.8 27.7 all-gather.8
  175.3 27.7 all-gather.6

commit v2 on v1

v2 whole, which is shorter than its diff:
```python
import jax
import jax.numpy as jnp
from jax import lax
from jax.experimental import pallas as pl
from jax.experimental.pallas import tpu as pltpu
from jax.sharding import PartitionSpec as P


MOST = 4


def column_tile(columns):
    for tile in (512, 384, 256, 128):
        if columns % tile == 0:
            return tile
    return columns


def stream_kernel(place, rows, slots, contributions, out):
    row_total = rows.shape[0]
    token = place[0] * row_total + lax.broadcasted_iota(
        jnp.int32, (row_total, slots.shape[1]), 0
    )
    table = (token == slots[...]).astype(jnp.bfloat16)
    added = jnp.dot(table, contributions[0], preferred_element_type=jnp.float32)
    out[...] = (rows[...].astype(jnp.float32) + added).astype(jnp.bfloat16)


def make_stream(residual, place, token_of_slot, contributions):
    blocks, slots, part = contributions.shape
    row_total, width = residual.shape
    return pl.pallas_call(
        stream_kernel,
        grid_spec=pltpu.PrefetchScalarGridSpec(
            num_scalar_prefetch=1,
            grid=(blocks,),
            in_specs=[
                pl.BlockSpec((row_total, part), lambda t, p: (0, t)),
                pl.BlockSpec((1, slots), lambda t, p: (0, 0)),
                pl.BlockSpec((1, slots, part), lambda t, p: (p[0] ^ t, 0, 0)),
            ],
            out_specs=pl.BlockSpec((row_total, part), lambda t, p: (0, t)),
        ),
        out_shape=jax.ShapeDtypeStruct((row_total, width), jnp.bfloat16),
        cost_estimate=pl.CostEstimate(
            flops=2 * row_total * slots * width, bytes_accessed=4 << 20, transcendentals=0
        ),
        name="stream_rows",
    )(place, residual, token_of_slot, contributions)


def project_pair(place, first, second, token_of_slot, contributions, gain, weights, target):
    blocks, slots, part = contributions.shape
    tok_rows, width = first.shape
    columns = weights.shape[1]
    tile = column_tile(columns)

    def kernel(place_ref, a_ref, b_ref, slots_ref, contributions_ref, gain_ref, w_ref, *rest):
        out, combined, normed = rest[-3:]
        me = place_ref[0]
        owner = place_ref[1]

        @pl.when(pl.program_id(0) == 0)
        def _():
            row = lax.broadcasted_iota(jnp.int32, (tok_rows, slots), 0)
            for h, rows_ref in enumerate((a_ref, b_ref)):
                down = slice(h * tok_rows, (h + 1) * tok_rows)
                table = (row + (owner ^ h) * tok_rows == slots_ref[...]).astype(jnp.bfloat16)
                squares = jnp.zeros((tok_rows, 1), jnp.float32)
                for t in range(blocks):
                    at = slice(t * part, (t + 1) * part)
                    value = rows_ref[:, at].astype(jnp.float32) + jnp.dot(
                        table, contributions_ref[me ^ t], preferred_element_type=jnp.float32
                    )
                    combined[down, at] = value
                    squares = squares + jnp.sum(value * value, axis=1, keepdims=True)
                scale = lax.rsqrt(squares / width + 1e-06)
                for t in range(blocks):
                    at = slice(t * part, (t + 1) * part)
                    normed[down, at] = (combined[down, at] * scale * gain_ref[:, at]).astype(
                        jnp.bfloat16
                    )

        value = jnp.dot(normed[...], w_ref[...], preferred_element_type=jnp.float32)
        value = value.astype(jnp.bfloat16)
        odd = owner % 2
        out[odd] = value[:tok_rows]
        out[1 - odd] = value[tok_rows:]

    in_specs = [
        pl.BlockSpec((tok_rows, width), lambda n, p: (0, 0)),
        pl.BlockSpec((tok_rows, width), lambda n, p: (0, 0)),
        pl.BlockSpec((1, slots), lambda n, p: (0, 0)),
        pl.BlockSpec((blocks, slots, part), lambda n, p: (0, 0, 0)),
        pl.BlockSpec((1, width), lambda n, p: (0, 0)),
        pl.BlockSpec((width, tile), lambda n, p: (0, n)),
    ]
    operands = [place, first, second, token_of_slot, contributions, gain, weights]
    aliases = {}
    if target is not None:
        in_specs.append(pl.BlockSpec(memory_space=pl.ANY))
        operands.append(target)
        aliases = {7: 0}
    return pl.pallas_call(
        kernel,
        grid_spec=pltpu.PrefetchScalarGridSpec(
            num_scalar_prefetch=1,
            grid=(columns // tile,),
            in_specs=in_specs,
            out_specs=pl.BlockSpec((2, tok_rows, tile), lambda n, p: (p[1] // 2, 0, n)),
            scratch_shapes=[
                pltpu.VMEM((2 * tok_rows, width), jnp.float32),
                pltpu.VMEM((2 * tok_rows, width), jnp.bfloat16),
            ],
        ),
        out_shape=jax.ShapeDtypeStruct((blocks, tok_rows, columns), jnp.bfloat16),
        input_output_aliases=aliases,
        cost_estimate=pl.CostEstimate(
            flops=4 * tok_rows * width * (columns + slots),
            bytes_accessed=2 * width * columns,
            transcendentals=0,
        ),
        compiler_params=pltpu.CompilerParams(vmem_limit_bytes=58 << 20),
        name="project_rows",
    )(*operands)


def from_partner(value, count, apart):
    return lax.ppermute(value, "tensor", [(d, d ^ apart) for d in range(count)])


def gather_pairs(value, count):
    pairs = []
    for k in range(0, count, 2):
        near = value if k == 0 else from_partner(value, count, k)
        pairs.append((near, from_partner(near, count, 1)))
    return pairs


def layer(
    expert_inputs, gates, chosen_tokens, w_gate, w_up, w_down, residual, norm_gain, w_qkv
):
    expert_count = lax.axis_size("expert")
    tensor_count = lax.axis_size("tensor")
    group_index = lax.axis_index("expert")
    tensor_index = lax.axis_index("tensor")
    local_experts, slot_count, feature_width = expert_inputs.shape
    tok_rows = residual.shape[0]
    group_rows = tok_rows * tensor_count
    total_experts = expert_count * local_experts
    local_rows = local_experts * slot_count
    feature_part = feature_width // tensor_count

    gathered = gather_pairs(residual, tensor_count)

    in_group = (chosen_tokens // group_rows) == group_index
    rank = jnp.cumsum(in_group.astype(jnp.int32), axis=1) - 1
    per_expert = min(MOST * tensor_count, slot_count)
    compact_rows = total_experts * per_expert
    slot = jnp.where(
        in_group,
        jnp.arange(total_experts, dtype=jnp.int32)[:, None] * per_expert + rank,
        compact_rows,
    ).reshape(-1)
    pick = jnp.arange(compact_rows, dtype=jnp.int32)[:, None] == slot[None, :]
    local_token = (chosen_tokens % group_rows).reshape(-1)
    token_of_slot = jnp.sum(jnp.where(pick, local_token[None, :] + 1, 0), axis=1) - 1
    pick = pick.astype(jnp.bfloat16)

    gate_part = jnp.einsum(
        "ecd,edf->ecf", expert_inputs, w_gate, preferred_element_type=jnp.float32
    )
    up_part = jnp.einsum("ecd,edf->ecf", expert_inputs, w_up, preferred_element_type=jnp.float32)
    hidden = (jax.nn.silu(gate_part) * up_part).astype(jnp.bfloat16)
    partial_value = (
        jnp.einsum("ecf,efd->ecd", hidden, w_down, preferred_element_type=jnp.float32)
        * gates[:, :, None]
    ).astype(jnp.bfloat16)
    partial_rows = partial_value.reshape(local_rows, feature_width)

    blocks = lax.all_to_all(
        partial_rows, "tensor", split_axis=1, concat_axis=0, tiled=True
    ).reshape(tensor_count, local_rows, feature_part)
    summed = lax.optimization_barrier(jnp.sum(blocks.astype(jnp.float32), axis=0))
    every_row = lax.all_gather(summed.astype(jnp.bfloat16), "expert", axis=0, tiled=True)
    compact = jnp.dot(pick, every_row, preferred_element_type=jnp.float32).astype(jnp.bfloat16)
    shared = [piece for pair in gather_pairs(compact, tensor_count) for piece in pair]
    contributions = jnp.stack(shared)

    slots = token_of_slot.reshape(1, compact_rows)
    gain = norm_gain.reshape(1, feature_width)
    me = tensor_index.astype(jnp.int32)
    stream = make_stream(residual, me.reshape(1), slots, contributions)
    projected = None
    for k in range(0, tensor_count, 2):
        place = jnp.stack([me, me ^ k])
        projected = project_pair(
            place, *gathered[k // 2], slots, contributions, gain, w_qkv, projected
        )
    return (stream, projected.reshape(group_rows, -1))


def solution(mesh):
    return jax.shard_map(
        layer,
        mesh=mesh,
        in_specs=(
            P("expert", None, None),
            P("expert", None),
            P(),
            P("expert", None, "tensor"),
            P("expert", None, "tensor"),
            P("expert", "tensor", None),
            P(("expert", "tensor"), None),
            P(),
            P(None, "tensor"),
        ),
        out_specs=(P(("expert", "tensor"), None), P("expert", "tensor")),
        check_vma=False,
    )
```

time: 221 us -> 155 us (0.70)
  waiting for transfers between devices: 122 us -> 55 us
  between operations: 13.9 us -> 0.78 us
  starting transfers between devices: 5.57 us -> 14.8 us
  Pallas kernels: 47.3 us -> 50.3 us
  other arithmetic: 1.12 us -> 3.62 us
    all_gather x5 -> x0, waiting for transfers between devices: 106 us -> none  [the longest x4 82.1 us: layer(): gathered.append(lax.all_gather(piece, 'tensor', axis=0, tiled=True))]
    all_to_all x1, waiting for transfers between devices: 14.9 us -> 40.8 us  [layer(): lax.all_to_all(partial_rows, 'tensor', split_axis=1, concat_axis=0, tiled...]
    ppermute x0 -> x14, waiting for transfers between devices: none -> 14.2 us  [from_partner(): return lax.ppermute(value, 'tensor', [(d, d ^ apart) for d in range(count)])]
    ppermute x0 -> x14, starting transfers between devices: none -> 10.6 us  [from_partner(): return lax.ppermute(value, 'tensor', [(d, d ^ apart) for d in range(count)])]
    pallas_call x5, Pallas kernels: 47.3 us -> 50.3 us  [the longest x4 43.9 us: project_pair(): pl.pallas_call(kernel, grid_spec=pltpu.PrefetchScalarGridSpec(num_scalar_...]
    another operation x0 -> x4, other arithmetic: none -> 2.47 us  [layer(): place = jnp.stack([me, me ^ k])]
  transfers between devices with their start and end apart: 6 -> 15, of which waited for: 6 -> 5; matrix products, arithmetic and copies ran while one was open for 1% -> 10% of each run, Pallas kernels for 17% -> 25%
where the time goes in v2:
time: 155 us
  waiting for transfers between devices  55 us (35%)
  Pallas kernels  50.3 us (32%)
  blocking collectives  16.4 us (11%)
  starting transfers between devices  14.8 us (10%)
  matrix products  9.47 us (6%)
  local copies, waits for them, and re-layouts  4.25 us (3%)
  other arithmetic  3.62 us (2%)
    pallas_call x4, Pallas kernels, project_pair(): pl.pallas_call(kernel, grid_spec=pltpu.PrefetchScalarGridSpec(num_scalar_...  43.9 us
    all_to_all x1, waiting for transfers between devices, layer(): lax.all_to_all(partial_rows, 'tensor', split_axis=1, concat_axis=0, tiled...  40.8 us
    all_gather x1, blocking collectives, layer(): lax.all_gather(summed.astype(jnp.bfloat16), 'expert', axis=0, tiled=True)  16.4 us
    ppermute x14, waiting for transfers between devices, from_partner(): return lax.ppermute(value, 'tensor', [(d, d ^ apart) for d in range(count)])  14.2 us
    ppermute x14, starting transfers between devices, from_partner(): return lax.ppermute(value, 'tensor', [(d, d ^ apart) for d in range(count)])  10.6 us
    pallas_call x1, Pallas kernels, make_stream(): pl.pallas_call(stream_kernel, grid_spec=pltpu.PrefetchScalarGridSpec(num_...  6.37 us
    dot_general x1, matrix products, layer(): jnp.einsum('ecf,efd->ecd', hidden, w_down, preferred_element_type=jnp.flo...  5.15 us
    all_to_all x1, starting transfers between devices, layer(): lax.all_to_all(partial_rows, 'tensor', split_axis=1, concat_axis=0, tiled...  4.18 us
  transfers between devices with their start and end apart: 15, of which 5 were waited for; matrix products, arithmetic and copies ran while one was open for 10% of the time, Pallas kernels for 25%

profile of v2, /device:TPU:0, one launch (start us, length us, event | category | flops | bytes accessed | tf_op | source)
XLA Modules:
  0.0 154.6 jit_solution(9392385592766199182)
XLA Ops:
  0.7 3.0 %collective-permute-start.11 = (bf16[128,4096]{1,0:T(8,128)(2,1)}, bf16[128,4096]{1,0:T(8,128)(2,1)}, u32[]{:S(2)}, u32[]{:S(2)}) collective-permute-start(bf16[128,4096]{1,0:T(8,128)(2,1)} %a_ref.1), channel_id=1, source_target_pairs={{0,2},{1,3},{2,0},{3,1},{4,6},{5,7},{6,4},{7,5},{8,10},{9,11},{10,... | collective-permute-start | bytes 3145736 | tf_op jit(solution)/shard_map/ppermute | solution.py:129
  3.7 1.5 collective-permute-start.9
  5.2 3.3 %fusion.16 = f32[2,64,224]{2,1,0:T(8,128)S(1)} fusion(bf16[2,64,4096]{2,1,0:T(8,128)(2,1)S(1)} %copy-done, bf16[2,4096,224]{1,2,0:T(8,128)(2,1)} %param.12), kind=kOutput, calls=%fused_computation.42 | convolution fusion | flops 234881024 | bytes 4833280 | tf_op jit(solution)/shard_map/ecd,edf->ecf/dot_general | solution.py:170
  8.5 5.2 %fusion = bf16[2,64,4096]{2,1,0:T(8,128)(2,1)S(1)} fusion(bf16[2,224,4096]{2,1,0:T(8,128)(2,1)} %param.14, bf16[2,64,4096]{2,1,0:T(8,128)(2,1)S(1)} %copy-done, bf16[2,4096,224]{1,2,0:T(8,128)(2,1)} %param.13, f32[2,64]{1,0:T(2,128)S(1)} %copy-done.3, f32[2,64,224]{2,1,0:T(8,128)S(1)} %fusion.16), kind=kOutput, calls=%fused_computation.1 | convolution fusion | flops 470982656 | bytes 9552384 | tf_op jit(solution)/shard_map/ecf,efd->ecd/dot_general | solution.py:176
  14.1 1.3 copy.15
  15.4 4.2 %all-to-all-start = ((bf16[128,8,512]{2,0,1:T(8,128)(2,1)}), bf16[128,8,512]{2,0,1:T(8,128)(2,1)S(1)}, u32[]{:S(2)}, u32[]{:S(2)}) async-start(bf16[128,8,512]{2,0,1:T(8,128)(2,1)} %copy.15), calls=%async_computation | async-start | bytes 2097152 | tf_op jit(solution)/shard_map/all_to_all | solution.py:181
  20.1 0.6 pad_add_fusion.3.place_ref
  21.4 40.8 %all-to-all-done = bf16[128,8,512]{2,0,1:T(8,128)(2,1)S(1)} async-done(((bf16[128,8,512]{2,0,1:T(8,128)(2,1)}), bf16[128,8,512]{2,0,1:T(8,128)(2,1)S(1)}, u32[]{:S(2)}, u32[]{:S(2)}) %all-to-all-start) | async-done | bytes 1048608 | tf_op jit(solution)/shard_map/all_to_all | solution.py:181
  62.4 16.4 %all_gather.3 = bf16[512,512]{1,0:T(8,128)(2,1)S(1)} all-gather(bf16[128,512]{1,0:T(8,128)(2,1)S(1)} %convert_reduce_fusion), channel_id=1, replica_groups=mesh['expert'=4,'tensor'=8] {'expert'}, dimensions={0}, use_global_device_ids=true | all-gather | bytes 655360 | tf_op jit(solution)/shard_map/all_gather | solution.py:185
  78.8 1.0 bitcast_dynamic-update-slice_fusion.7
  79.9 0.7 pad_add_fusion.2.place_ref
  81.1 0.6 pad_add_fusion.place_ref
  81.8 1.4 collective-permute-start.3
  83.2 5.5 %collective-permute-done.1 = bf16[256,512]{1,0:T(8,128)(2,1)S(1)} collective-permute-done((bf16[256,512]{1,0:T(8,128)(2,1)}, bf16[256,512]{1,0:T(8,128)(2,1)S(1)}, u32[]{:S(2)}, u32[]{:S(2)}) %collective-permute-start.1) | collective-permute-done | bytes 262176 | tf_op jit(solution)/shard_map/ppermute | solution.py:129
  88.7 1.0 bitcast_dynamic-update-slice_fusion.6
  90.6 2.7 %collective-permute-start.5 = (bf16[256,512]{1,0:T(8,128)(2,1)}, bf16[256,512]{1,0:T(8,128)(2,1)S(1)}, u32[]{:S(2)}, u32[]{:S(2)}) collective-permute-start(bf16[256,512]{1,0:T(8,128)(2,1)} %get-tuple-element.5), channel_id=1, source_target_pairs={{0,6},{1,7},{2,4},{3,5},{4,2},{5,3},{6,0},{7,1},{8,14},{9,15},{10,... | collective-permute-start | bytes 786440 | tf_op jit(solution)/shard_map/ppermute | solution.py:129
  94.0 5.7 %collective-permute-done.5 = bf16[256,512]{1,0:T(8,128)(2,1)S(1)} collective-permute-done((bf16[256,512]{1,0:T(8,128)(2,1)}, bf16[256,512]{1,0:T(8,128)(2,1)S(1)}, u32[]{:S(2)}, u32[]{:S(2)}) %collective-permute-start.5) | collective-permute-done | bytes 262176 | tf_op jit(solution)/shard_map/ppermute | solution.py:129
  100.3 2.7 %collective-permute-done.6 = bf16[256,512]{1,0:T(8,128)(2,1)S(1)} collective-permute-done((bf16[256,512]{1,0:T(8,128)(2,1)S(1)}, bf16[256,512]{1,0:T(8,128)(2,1)S(1)}, u32[]{:S(2)}, u32[]{:S(2)}) %collective-permute-start.6) | collective-permute-done | bytes 262176 | tf_op jit(solution)/shard_map/ppermute | solution.py:129
  103.0 1.3 copy-done.1
  104.3 6.4 %stream_rows.1 = bf16[128,4096]{1,0:T(8,128)(2,1)} custom-call(s32[1]{0:T(128)} %bitcast.place, bf16[128,4096]{1,0:T(8,128)(2,1)} %a_ref.1, s32[1,256]{1,0:T(1,128)} %bitcast.39, bf16[8,256,512]{2,1,0:T(8,128)(2,1)} %copy-done.1), custom_call_target="tpu_custom_call" | custom-call | flops 268435456 | bytes 4194304 | tf_op jit(solution)/shard_map/stream_rows/pallas_call | solution.py:32
  110.7 11.0 %project_rows.4.rest_0_ = bf16[8,128,1536]{2,1,0:T(8,128)(2,1)} custom-call(s32[2]{0:T(128)} %pad_add_fusion.3.place_ref, bf16[128,4096]{1,0:T(8,128)(2,1)} %a_ref.1, bf16[128,4096]{1,0:T(8,128)(2,1)} %collective-permute-done.13.b_ref, s32[1,256]{1,0:T(1,128)} %bitcast.40, bf16[8,256,512]{2,1,0:T(8,128)(2,1)} %copy-done.1, f32[1,4096]{1,0:T(1,128)} %bitcast.35, ...), custom_call_target="tpu_custom_call" | custom-call | flops 3758096384 | bytes 12582912 | tf_op jit(solution)/shard_map/project_rows/pallas_call | solution.py:104
  121.7 11.0 %project_rows.5.rest_0_ = bf16[8,128,1536]{2,1,0:T(8,128)(2,1)} custom-call(s32[2]{0:T(128)} %pad_add_fusion.2.place_ref, bf16[128,4096]{1,0:T(8,128)(2,1)} %collective-permute-done.11.a_ref, bf16[128,4096]{1,0:T(8,128)(2,1)} %collective-permute-done.12.b_ref, s32[1,256]{1,0:T(1,128)} %bitcast.41, ...), custom_call_target="tpu_custom_call", output_to_operand_aliasing={{}: (7, {})} | custom-call | flops 3758096384 | bytes 12582912 | tf_op jit(solution)/shard_map/project_rows/pallas_call | solution.py:104
  132.6 11.0 %project_rows.6.rest_0_ = bf16[8,128,1536]{2,1,0:T(8,128)(2,1)} custom-call(s32[2]{0:T(128)} %pad_add_fusion.1.place_ref, bf16[128,4096]{1,0:T(8,128)(2,1)} %collective-permute-done.9.a_ref, bf16[128,4096]{1,0:T(8,128)(2,1)} %collective-permute-done.10.b_ref, s32[1,256]{1,0:T(1,128)} %bitcast.42, ...), custom_call_target="tpu_custom_call", output_to_operand_aliasing={{}: (7, {})} | custom-call | flops 3758096384 | bytes 12582912 | tf_op jit(solution)/shard_map/project_rows/pallas_call | solution.py:104
  143.6 11.0 %project_rows.7 = bf16[8,128,1536]{2,1,0:T(8,128)(2,1)} custom-call(s32[2]{0:T(128)} %pad_add_fusion.place_ref, bf16[128,4096]{1,0:T(8,128)(2,1)} %collective-permute-done.7.a_ref, bf16[128,4096]{1,0:T(8,128)(2,1)} %collective-permute-done.8.b_ref, s32[1,256]{1,0:T(1,128)} %bitcast.43, ...), custom_call_target="tpu_custom_call", output_to_operand_aliasing={{}: (7, {})} | custom-call | flops 3758096384 | bytes 12582912 | tf_op jit(solution)/shard_map/project_rows/pallas_call | solution.py:104
  (46 shorter events, 4.6 us)
Async XLA Ops:
  0.6 4.6 %copy-start = (bf16[2,64,4096]{2,1,0:T(8,128)(2,1)S(1)}, bf16[2,64,4096]{2,1,0:T(8,128)(2,1)}, u32[]{:S(2)}) copy-start(bf16[2,64,4096]{2,1,0:T(8,128)(2,1)} %param.9) | copy-start | bytes 3145732
  0.6 7.9 %copy-start.3 = (f32[2,64]{1,0:T(2,128)S(1)}, f32[2,64]{1,0:T(2,128)}, u32[]{:S(2)}) copy-start(f32[2,64]{1,0:T(2,128)} %param.10) | copy-start | bytes 1540
  0.7 89.1 %collective-permute-start.11 = (bf16[128,4096]{1,0:T(8,128)(2,1)}, bf16[128,4096]{1,0:T(8,128)(2,1)}, u32[]{:S(2)}, u32[]{:S(2)}) collective-permute-start(bf16[128,4096]{1,0:T(8,128)(2,1)} %a_ref.1), channel_id=1, source_target_pairs={{0,2},{1,3},{2,0},{3,1},{4,6},{5,7},{6,4},{7,5},{8,10},{9,11},{10,... | collective-permute-start | bytes 3145736 | tf_op jit(solution)/shard_map/ppermute | solution.py:129
  3.7 89.6 %collective-permute-start.9 = (bf16[128,4096]{1,0:T(8,128)(2,1)}, bf16[128,4096]{1,0:T(8,128)(2,1)}, u32[]{:S(2)}, u32[]{:S(2)}) collective-permute-start(bf16[128,4096]{1,0:T(8,128)(2,1)} %a_ref.1), channel_id=1, source_target_pairs={{0,4},{1,5},{2,6},{3,7},{4,0},{5,1},{6,2},{7,3},{8,12},{9,13},{10,... | collective-permute-start | bytes 3145736 | tf_op jit(solution)/shard_map/ppermute | solution.py:129
  5.2 88.7 %collective-permute-start.7 = (bf16[128,4096]{1,0:T(8,128)(2,1)}, bf16[128,4096]{1,0:T(8,128)(2,1)}, u32[]{:S(2)}, u32[]{:S(2)}) collective-permute-start(bf16[128,4096]{1,0:T(8,128)(2,1)} %a_ref.1), channel_id=1, source_target_pairs={{0,6},{1,7},{2,4},{3,5},{4,2},{5,3},{6,0},{7,1},{8,14},{9,15},{10,... | collective-permute-start | bytes 3145736 | tf_op jit(solution)/shard_map/ppermute | solution.py:129
  14.1 5.5 %copy-start.2 = (s32[8,64]{1,0:T(8,128)S(1)}, s32[8,64]{1,0:T(8,128)}, u32[]{:S(2)}) copy-start(s32[8,64]{1,0:T(8,128)} %param.11) | copy-start | bytes 6148
  15.4 46.8 %all-to-all-start = ((bf16[128,8,512]{2,0,1:T(8,128)(2,1)}), bf16[128,8,512]{2,0,1:T(8,128)(2,1)S(1)}, u32[]{:S(2)}, u32[]{:S(2)}) async-start(bf16[128,8,512]{2,0,1:T(8,128)(2,1)} %copy.15), calls=%async_computation | async-start | bytes 2097152 | tf_op jit(solution)/shard_map/all_to_all | solution.py:181
  79.8 2.0 %collective-permute-start = (bf16[256,512]{1,0:T(8,128)(2,1)}, bf16[256,512]{1,0:T(8,128)(2,1)}, u32[]{:S(2)}, u32[]{:S(2)}) collective-permute-start(bf16[256,512]{1,0:T(8,128)(2,1)} %get-tuple-element.5), channel_id=1, source_target_pairs={{0,1},{1,0},{2,3},{3,2},{4,5},{5,4},{6,7},{7,6},{8,9},{9,8},{10,11... | collective-permute-start | bytes 786440 | tf_op jit(solution)/shard_map/ppermute | solution.py:129
  79.8 8.9 %collective-permute-start.1 = (bf16[256,512]{1,0:T(8,128)(2,1)}, bf16[256,512]{1,0:T(8,128)(2,1)S(1)}, u32[]{:S(2)}, u32[]{:S(2)}) collective-permute-start(bf16[256,512]{1,0:T(8,128)(2,1)} %get-tuple-element.5), channel_id=1, source_target_pairs={{0,2},{1,3},{2,0},{3,1},{4,6},{5,7},{6,4},{7,5},{8,10},{9,11},{10,... | collective-permute-start | bytes 786440 | tf_op jit(solution)/shard_map/ppermute | solution.py:129
  81.8 8.8 %collective-permute-start.3 = (bf16[256,512]{1,0:T(8,128)(2,1)}, bf16[256,512]{1,0:T(8,128)(2,1)S(1)}, u32[]{:S(2)}, u32[]{:S(2)}) collective-permute-start(bf16[256,512]{1,0:T(8,128)(2,1)} %get-tuple-element.5), channel_id=1, source_target_pairs={{0,4},{1,5},{2,6},{3,7},{4,0},{5,1},{6,2},{7,3},{8,12},{9,13},{10,... | collective-permute-start | bytes 786440 | tf_op jit(solution)/shard_map/ppermute | solution.py:129
  88.7 4.5 %collective-permute-start.2 = (bf16[256,512]{1,0:T(8,128)(2,1)S(1)}, bf16[256,512]{1,0:T(8,128)(2,1)S(1)}, u32[]{:S(2)}, u32[]{:S(2)}) collective-permute-start(bf16[256,512]{1,0:T(8,128)(2,1)S(1)} %collective-permute-done.1), channel_id=1, source_target_pairs={{0,1},{1,0},{2,3},{3,2},{4,5},{5,4},{6,7},{7,6},{8,9},{9,8},{10,11... | collective-permute-start | bytes 786440 | tf_op jit(solution)/shard_map/ppermute | solution.py:129
  89.7 21.0 %collective-permute-start.13 = (bf16[128,4096]{1,0:T(8,128)(2,1)}, bf16[128,4096]{1,0:T(8,128)(2,1)}, u32[]{:S(2)}, u32[]{:S(2)}) collective-permute-start(bf16[128,4096]{1,0:T(8,128)(2,1)} %a_ref.1), channel_id=1, source_target_pairs={{0,1},{1,0},{2,3},{3,2},{4,5},{5,4},{6,7},{7,6},{8,9},{9,8},{10,11... | collective-permute-start | bytes 3145736 | tf_op jit(solution)/shard_map/ppermute | solution.py:129
  90.6 9.2 %collective-permute-start.5 = (bf16[256,512]{1,0:T(8,128)(2,1)}, bf16[256,512]{1,0:T(8,128)(2,1)S(1)}, u32[]{:S(2)}, u32[]{:S(2)}) collective-permute-start(bf16[256,512]{1,0:T(8,128)(2,1)} %get-tuple-element.5), channel_id=1, source_target_pairs={{0,6},{1,7},{2,4},{3,5},{4,2},{5,3},{6,0},{7,1},{8,14},{9,15},{10,... | collective-permute-start | bytes 786440 | tf_op jit(solution)/shard_map/ppermute | solution.py:129
  93.3 6.5 %collective-permute-start.4 = (bf16[256,512]{1,0:T(8,128)(2,1)S(1)}, bf16[256,512]{1,0:T(8,128)(2,1)S(1)}, u32[]{:S(2)}, u32[]{:S(2)}) collective-permute-start(bf16[256,512]{1,0:T(8,128)(2,1)S(1)} %collective-permute-done.3), channel_id=1, source_target_pairs={{0,1},{1,0},{2,3},{3,2},{4,5},{5,4},{6,7},{7,6},{8,9},{9,8},{10,11... | collective-permute-start | bytes 786440 | tf_op jit(solution)/shard_map/ppermute | solution.py:129
  93.3 28.3 %collective-permute-start.12 = (bf16[128,4096]{1,0:T(8,128)(2,1)}, bf16[128,4096]{1,0:T(8,128)(2,1)}, u32[]{:S(2)}, u32[]{:S(2)}) collective-permute-start(bf16[128,4096]{1,0:T(8,128)(2,1)} %collective-permute-done.11.a_ref), channel_id=1, source_target_pairs={{0,1},{1,0},{2,3},{3,2},{4,5},{5,4},{6,7},{7,6},{8,9},{9,8},{10,11... | collective-permute-start | bytes 3145736 | tf_op jit(solution)/shard_map/ppermute | solution.py:129
  93.9 38.7 %collective-permute-start.10 = (bf16[128,4096]{1,0:T(8,128)(2,1)}, bf16[128,4096]{1,0:T(8,128)(2,1)}, u32[]{:S(2)}, u32[]{:S(2)}) collective-permute-start(bf16[128,4096]{1,0:T(8,128)(2,1)} %collective-permute-done.9.a_ref), channel_id=1, source_target_pairs={{0,1},{1,0},{2,3},{3,2},{4,5},{5,4},{6,7},{7,6},{8,9},{9,8},{10,11... | collective-permute-start | bytes 3145736 | tf_op jit(solution)/shard_map/ppermute | solution.py:129
  99.7 43.9 %collective-permute-start.8 = (bf16[128,4096]{1,0:T(8,128)(2,1)}, bf16[128,4096]{1,0:T(8,128)(2,1)}, u32[]{:S(2)}, u32[]{:S(2)}) collective-permute-start(bf16[128,4096]{1,0:T(8,128)(2,1)} %collective-permute-done.7.a_ref), channel_id=1, source_target_pairs={{0,1},{1,0},{2,3},{3,2},{4,5},{5,4},{6,7},{7,6},{8,9},{9,8},{10,11... | collective-permute-start | bytes 3145736 | tf_op jit(solution)/shard_map/ppermute | solution.py:129
  99.7 3.2 %collective-permute-start.6 = (bf16[256,512]{1,0:T(8,128)(2,1)S(1)}, bf16[256,512]{1,0:T(8,128)(2,1)S(1)}, u32[]{:S(2)}, u32[]{:S(2)}) collective-permute-start(bf16[256,512]{1,0:T(8,128)(2,1)S(1)} %collective-permute-done.5), channel_id=1, source_target_pairs={{0,1},{1,0},{2,3},{3,2},{4,5},{5,4},{6,7},{7,6},{8,9},{9,8},{10,11... | collective-permute-start | bytes 786440 | tf_op jit(solution)/shard_map/ppermute | solution.py:129
  103.0 1.3 copy-start.1
